TPU v7x, 32 devices: a whole 2x2x4 slice. The times are simulated.
32 devices in a mesh: rep: 4 (over y, x), fsdp: 8 (over z, core).
Axes of the slice: x: 2, y: 2, z: 4, core: 2. Of those that a mesh axis runs over, the one named last changes fastest.
Arguments:
- momentum: float32 [4, 18432, 2304], P('rep', 'fsdp'), may hold values from -60 to 60
- gradient: bfloat16 [4, 18432, 2304], P('rep', 'fsdp'), may hold values from -30 to 30
- right_factor: float32 [2304, 256], P('fsdp'), may hold values from -0.125 to 0.125
Outputs:
- new_momentum: float32 [4, 18432, 2304], P('rep', 'fsdp')
- update: bfloat16 [18432, 2304], P('fsdp')
- new_factor: float32 [2304, 256], P('fsdp')
All inputs are finite; a program needn't handle non-finite values.
Results may differ from a plain program's by a relative error of at most 0.001.
Values sent between devices are 32-bit elements; how exact they have to be, the bound alone decides.
A program may use at most 128 MiB of HBM per device.

v0:
```python
import math
import jax
import jax.numpy as jnp
from jax import lax
from jax.sharding import PartitionSpec as P

ROWS = 18432
COLS = 2304
RANK = 256
epsilon = 1e-06
decay_rate = 0.95
highest = lax.Precision.HIGHEST


def shards(momentum, gradient, right_factor):
    buffer = momentum[0] + gradient[0].astype(jnp.float32)
    replicas = lax.axis_size("rep")
    columns = buffer
    partial_left = jnp.dot(
        columns,
        lax.all_gather(right_factor, "fsdp", axis=0, tiled=True),
        precision=highest,
        preferred_element_type=jnp.float32,
    )
    projected = lax.psum(partial_left, "rep")
    local_gram = jnp.dot(
        projected.T, projected, precision=highest, preferred_element_type=jnp.float32
    )
    gram_matrix = lax.psum(local_gram, "fsdp")
    lower_factor = jnp.linalg.cholesky(gram_matrix)
    orthonormal = jax.scipy.linalg.solve_triangular(lower_factor, projected.T, lower=True).T
    columns = buffer
    scattered = lax.psum_scatter(
        lax.dot_general(
            columns,
            orthonormal,
            (((0,), (0,)), ((), ())),
            precision=highest,
            preferred_element_type=jnp.float32,
        ),
        "fsdp",
        scatter_dimension=0,
        tiled=True,
    )
    own_factor = lax.psum(scattered, "rep") / replicas
    full_factor = lax.all_gather(own_factor, "fsdp", axis=0, tiled=True)
    col_norms = jnp.sqrt(jnp.sum(full_factor * full_factor, axis=0) + epsilon)
    new_factor = own_factor / col_norms
    correction = lax.dot_general(
        orthonormal,
        full_factor,
        (((1,), (1,)), ((), ())),
        precision=highest,
        preferred_element_type=jnp.float32,
    )
    new_momentum = (buffer - (1.0 - decay_rate) * correction)[None]
    direction = lax.dot_general(
        orthonormal,
        full_factor / col_norms,
        (((1,), (1,)), ((), ())),
        precision=highest,
        preferred_element_type=jnp.float32,
    )
    update = (math.sqrt(ROWS * COLS / RANK) * direction).astype(jnp.bfloat16)
    return (new_momentum, update, new_factor)


def solution(mesh):
    in_specs = (P("rep", "fsdp", None), P("rep", "fsdp", None), P("fsdp", None))
    out_specs = (P("rep", "fsdp", None), P("fsdp", None), P("fsdp", None))
    return jax.shard_map(shards, mesh=mesh, in_specs=in_specs, out_specs=out_specs, check_vma=False)
```

profile of v0, /device:TPU:0, one launch (start us, length us, event | category | flops | bytes accessed | tf_op | source)
XLA Modules:
  0.0 512.4 jit_solution(980822565762107197)
XLA Ops:
  7.9 35.9 %all-gather.3.cloned.1.call-done = f32[2304,256]{1,0:T(8,128)} async-done(((f32[288,256]{1,0:T(8,128)}), f32[2304,256]{1,0:T(8,128)}) %all-gather.3.cloned.1.call-update) | async-done | bytes 2359312 | tf_op jit(solution)/shard_map/all_gather | solution.py:21
  43.8 22.8 %fusion.3 = f32[2304,256]{1,0:T(8,128)} fusion(f32[2304,256]{1,0:T(8,128)} %all-gather.3.cloned.1.call-done, f32[1,2304,2304]{2,1,0:T(8,128)} %param.3, bf16[1,2304,2304]{2,1,0:T(8,128)(2,1)} %param.4), kind=kOutput, calls=%fused_computation.7 | convolution fusion | flops 16318070784 | bytes 36569088 | tf_op jit(solution)/shard_map/dot_general | solution.py:19
  66.7 73.2 %all-reduce.5.cloned.1.call-done = f32[2304,256]{1,0:T(8,128)} async-done(((f32[2304,256]{1,0:T(8,128)}), f32[2304,256]{1,0:T(8,128)}) %all-reduce.5.cloned.1.call-update) | async-done | bytes 2359312 | tf_op jit(solution)/shard_map/psum | solution.py:25
  139.9 6.9 %fusion.21 = f32[256,256]{0,1:T(8,128)} fusion(f32[2304,256]{1,0:T(8,128)} %all-reduce.5.cloned.1.call-done), kind=kOutput, calls=%fused_computation.48 | convolution fusion | flops 1811939328 | bytes 2621440 | tf_op jit(solution)/shard_map/dot_general | solution.py:26
  147.1 55.3 %all-reduce.7.cloned.1.call-done = f32[256,256]{0,1:T(8,128)} async-done(((f32[256,256]{0,1:T(8,128)}), f32[256,256]{0,1:T(8,128)}) %all-reduce.7.cloned.1.call-update) | async-done | bytes 262160 | tf_op jit(solution)/shard_map/psum | solution.py:29
  202.4 1.1 copy.7
  204.5 11.7 %cholesky.50 = f32[128,128]{1,0:T(8,128)S(1)} custom-call(f32[128,128]{1,0:T(8,128)S(1)} %cholesky.118), custom_call_target="Cholesky" | custom-call | tf_op jit(solution)/shard_map/jit(cholesky)/cholesky | solution.py:30
  216.3 9.8 %custom-call.15 = f32[1,128,128]{1,2,0:T(8,128)S(1)} custom-call(f32[1,128,128]{2,1,0:T(8,128)S(1)} %get-tuple-element.24), custom_call_target="InvertDiagBlocksLowerTriangular" | custom-call | tf_op jit(solution)/shard_map/jit(cholesky)/cholesky | solution.py:30
  226.6 11.7 %cholesky.105 = f32[128,128]{1,0:T(8,128)S(1)} custom-call(f32[128,128]{1,0:T(8,128)S(1)} %convolution_subtract_fusion.1), custom_call_target="Cholesky" | custom-call | tf_op jit(solution)/shard_map/jit(cholesky)/cholesky | solution.py:30
  240.4 4.4 while.1
  241.4 1.4 bitcast_dynamic-update-slice_fusion.2
  243.4 1.4 bitcast_dynamic-update-slice_fusion.2
  244.8 20.3 %custom-call.16 = f32[2,128,128]{1,2,0:T(8,128)} custom-call(f32[2,128,128]{2,1,0:T(8,128)S(1)} %get-tuple-element.10), custom_call_target="InvertDiagBlocksLowerTriangular" | custom-call | tf_op jit(solution)/shard_map/jit(_solve_triangular)/triangular_solve | solution.py:31
  265.1 2.0 fusion.8
  267.1 2.9 convolution_subtract_fusion
  270.0 1.2 fusion.13
  271.2 38.5 %fusion.1 = f32[2304,256]{1,0:T(8,128)} fusion(f32[1,2304,2304]{2,1,0:T(8,128)} %param.3, bf16[1,2304,2304]{2,1,0:T(8,128)(2,1)} %param.4, f32[128,2304]{1,0:T(8,128)S(1)} %fusion.13, f32[128,2304]{1,0:T(8,128)S(1)} %fusion.8), kind=kOutput, calls=%fused_computation.5 | convolution fusion | flops 16318660608 | bytes 36569088 | tf_op jit(solution)/shard_map/dot_general | solution.py:34
  309.7 36.2 %reduce-scatter.2.cloned.1.call-done = f32[288,256]{1,0:T(8,128)} async-done(((f32[2304,256]{1,0:T(8,128)}), f32[288,256]{1,0:T(8,128)}) %reduce-scatter.2.cloned.1.call-update) | async-done | bytes 294928 | tf_op jit(solution)/shard_map/reduce_scatter | solution.py:33
  346.0 45.0 %all-reduce.9.cloned.1.call-done = f32[288,256]{1,0:T(8,128)} async-done(((f32[288,256]{1,0:T(8,128)}), f32[288,256]{1,0:T(8,128)}) %all-reduce.9.cloned.1.call-update) | async-done | bytes 294928 | tf_op jit(solution)/shard_map/psum | solution.py:45
  391.0 1.8 broadcast_multiply_fusion
  392.8 31.8 %all-gather.5.cloned.1.call-done = f32[2304,256]{1,0:T(8,128)} async-done(((f32[288,256]{1,0:T(8,128)}), f32[2304,256]{1,0:T(8,128)}) %all-gather.5.cloned.1.call-update) | async-done | bytes 2359312 | tf_op jit(solution)/shard_map/all_gather | solution.py:46
  424.5 2.1 multiply_reduce_fusion
  427.4 36.8 %fusion.6 = bf16[2304,2304]{1,0:T(8,128)(2,1)} fusion(f32[2304,256]{1,0:T(8,128)} %all-gather.5.cloned.1.call-done, f32[128,2304]{1,0:T(8,128)S(1)} %fusion.13, f32[128,2304]{1,0:T(8,128)S(1)} %fusion.8, f32[256]{0:T(256)S(1)} %add_sqrt_fusion), kind=kOutput, calls=%fused_computation.11 | convolution fusion | flops 16319250432 | bytes 15336448 | tf_op jit(solution)/shard_map/dot_general | solution.py:57
  464.3 40.8 %fusion.5 = f32[1,2304,2304]{2,1,0:T(8,128)} fusion(f32[2304,256]{1,0:T(8,128)} %all-gather.5.cloned.1.call-done, f32[1,2304,2304]{2,1,0:T(8,128)} %param.3, bf16[1,2304,2304]{2,1,0:T(8,128)(2,1)S(1)} %bitcast.47, f32[128,2304]{1,0:T(8,128)S(1)} %fusion.13, f32[128,2304]{1,0:T(8,128)S(1)} %fusion.8), kind=kOutput, calls=%fused_computation.10 | convolution fusion | flops 16329277440 | bytes 57802752 | tf_op jit(solution)/shard_map/dot_general | solution.py:49
  (45 shorter events, 5.5 us)
Async XLA Ops:
  7.2 36.6 %all-gather.3.cloned.1.call-start = ((), (), s32[]{:S(2)}) async-start(), calls=%async_computation.1 | async-start | bytes 2654208 | tf_op jit(solution)/shard_map/all_gather | solution.py:21
  7.9 132.0 %all-reduce.5.cloned.1.call-start = ((), (), s32[]{:S(2)}) async-start(), calls=%async_computation.2 | async-start | bytes 4718592 | tf_op jit(solution)/shard_map/psum | solution.py:25
  66.6 135.8 %all-reduce.7.cloned.1.call-start = ((), (), s32[]{:S(2)}) async-start(), calls=%async_computation.3 | async-start | bytes 524288 | tf_op jit(solution)/shard_map/psum | solution.py:29
  146.8 118.3 %copy-start = (f32[2304,256]{1,0:T(8,128)S(1)}, f32[2304,256]{1,0:T(8,128)}, u32[]{:S(2)}) copy-start(f32[2304,256]{1,0:T(8,128)} %all-reduce.5.cloned.1.call-done) | copy-start | bytes 7077892
  146.9 199.1 %reduce-scatter.2.cloned.1.call-start = ((), (), s32[]{:S(2)}) async-start(), calls=%async_computation.4 | async-start | bytes 2654208 | tf_op jit(solution)/shard_map/reduce_scatter | solution.py:33
  244.8 20.3 %copy-start.1 = (f32[256,256]{1,0:T(8,128)}, f32[256,256]{1,0:T(8,128)S(1)}, u32[]{:S(2)}) copy-start(f32[256,256]{1,0:T(8,128)S(1)} %get-tuple-element.86) | copy-start | bytes 786436
  267.1 2.9 copy-start.3
  309.7 81.3 %all-reduce.9.cloned.1.call-start = ((), (), s32[]{:S(2)}) async-start(), calls=%async_computation.5 | async-start | bytes 589824 | tf_op jit(solution)/shard_map/psum | solution.py:45
  346.0 78.6 %all-gather.5.cloned.1.call-start = ((), (), s32[]{:S(2)}) async-start(), calls=%async_computation.6 | async-start | bytes 2654208 | tf_op jit(solution)/shard_map/all_gather | solution.py:46
  391.0 35.7 %copy-start.2 = (f32[288,256]{1,0:T(8,128)S(1)}, f32[288,256]{1,0:T(8,128)}, u32[]{:S(2)}) copy-start(f32[288,256]{1,0:T(8,128)} %all-reduce.9.cloned.1.call-done) | copy-start | bytes 884740
  424.5 39.7 %slice-start = ((s8[10616832]{0:T(1024)(128)(4,1)}), s8[4194304]{0:T(1024)(128)(4,1)S(1)}, s32[]{:S(2)}) async-start(s8[10616832]{0:T(1024)(128)(4,1)} %bitcast.46), calls=%async_computation.7 | async-start | bytes 8388608
  427.4 36.8 %slice-start.1 = ((s8[10616832]{0:T(1024)(128)(4,1)}), s8[4194304]{0:T(1024)(128)(4,1)S(1)}, s32[]{:S(2)}) async-start(s8[10616832]{0:T(1024)(128)(4,1)} %bitcast.46), calls=%async_computation.8 | async-start | bytes 8388608
  427.4 36.8 %slice-start.2 = ((s8[10616832]{0:T(1024)(128)(4,1)}), s8[2228224]{0:T(1024)(128)(4,1)S(1)}, s32[]{:S(2)}) async-start(s8[10616832]{0:T(1024)(128)(4,1)} %bitcast.46), calls=%async_computation.9 | async-start | bytes 4456448
Sparse Core Ops, SparseCore 0:
  9.6 34.1 all-gather.2
  66.8 73.0 all-reduce.4
  147.0 55.4 all-reduce.6
  309.8 36.0 reduce-scatter.1
  348.7 42.2 all-reduce.8
  393.1 31.4 all-gather.4
where the time goes:
time: 520 us; the launch traced here: 512 us
  waiting for transfers between devices  278 us (53%)
  matrix products  152 us (29%)
  other arithmetic  59.9 us (12%)
  between operations  16 us (3%)
    psum x1, waiting for transfers between devices, shards(): projected = lax.psum(partial_left, 'rep')  73.2 us
    psum x1, waiting for transfers between devices, shards(): gram_matrix = lax.psum(local_gram, 'fsdp')  55.3 us
    psum x1, waiting for transfers between devices, shards(): own_factor = lax.psum(scattered, 'rep') / replicas  45 us
    dot_general x1, matrix products, shards(): lax.dot_general(orthonormal, full_factor, (((1,), (1,)), ((), ())), preci...  40.8 us
    dot_general x1, matrix products, shards(): lax.dot_general(columns, orthonormal, (((0,), (0,)), ((), ())), precision...  38.5 us
    dot_general x1, matrix products, shards(): lax.dot_general(orthonormal, full_factor / col_norms, (((1,), (1,)), ((),...  36.8 us
    reduce_scatter x1, waiting for transfers between devices, shards(): lax.psum_scatter(lax.dot_general(columns, orthonormal, (((0,), (0,)), (()...  36.2 us
    all_gather x1, waiting for transfers between devices, shards(): lax.all_gather(right_factor, 'fsdp', axis=0, tiled=True)  35.9 us
  transfers between devices with their start and end apart: 6, of which 6 were waited for; matrix products, arithmetic and copies ran while one was open for 0% of the time, Pallas kernels for 0%

commit v1 on v0

--- a/solution.py
+++ b/solution.py
@@ -10,6 +10,16 @@
 epsilon = 1e-06
 decay_rate = 0.95
 highest = lax.Precision.HIGHEST
+
+
+def pass_along(shard, axis, dim):
+    size = lax.axis_size(axis)
+    held, blocks = (shard, [shard])
+    for _ in range(size - 1):
+        held = lax.ppermute(held, axis, [(i, (i + 1) % size) for i in range(size)])
+        blocks.insert(0, held)
+    merged = jnp.concatenate(blocks, axis=dim)
+    return jnp.roll(merged, (lax.axis_index(axis) + 1) * shard.shape[dim], axis=dim)
 
 
 def shards(momentum, gradient, right_factor):
@@ -43,7 +53,7 @@
         tiled=True,
     )
     own_factor = lax.psum(scattered, "rep") / replicas
-    full_factor = lax.all_gather(own_factor, "fsdp", axis=0, tiled=True)
+    full_factor = pass_along(own_factor, "fsdp", 0)
     col_norms = jnp.sqrt(jnp.sum(full_factor * full_factor, axis=0) + epsilon)
     new_factor = own_factor / col_norms
     correction = lax.dot_general(

time: 520 us -> 548 us (1.054)
  waiting for transfers between devices: 278 us -> 302 us
  local copies, waits for them, and re-layouts: 5.15 us -> 12.7 us
    ppermute x0 -> x7, waiting for transfers between devices: none -> 56 us  [pass_along(): held = lax.ppermute(held, axis, [(i, (i + 1) % size) for i in range(size)])]
    all_gather x1 -> x0, waiting for transfers between devices: 31.8 us -> none  [shards(): full_factor = lax.all_gather(own_factor, 'fsdp', axis=0, tiled=True)]
    unnamed x14 -> x30, local copies, waits for them, and re-layouts: 0.03 us -> 7.53 us
  transfers between devices with their start and end apart: 6 -> 12, of which waited for: 6 -> 12; matrix products, arithmetic and copies ran while one was open for 0% -> 0% of each run, Pallas kernels for 0% -> 0%
where the time goes in v1:
time: 548 us; the launch traced here: 541 us
  waiting for transfers between devices  302 us (55%)
  matrix products  151 us (28%)
  other arithmetic  57.5 us (10%)
  between operations  15.8 us (3%)
  local copies, waits for them, and re-layouts  12.7 us (2%)
    psum x1, waiting for transfers between devices, shards(): projected = lax.psum(partial_left, 'rep')  73.2 us
    ppermute x7, waiting for transfers between devices, pass_along(): held = lax.ppermute(held, axis, [(i, (i + 1) % size) for i in range(size)])  56 us
    psum x1, waiting for transfers between devices, shards(): gram_matrix = lax.psum(local_gram, 'fsdp')  55.3 us
    psum x1, waiting for transfers between devices, shards(): own_factor = lax.psum(scattered, 'rep') / replicas  45.1 us
    dot_general x1, matrix products, shards(): lax.dot_general(orthonormal, full_factor, (((1,), (1,)), ((), ())), preci...  40.8 us
    dot_general x1, matrix products, shards(): lax.dot_general(columns, orthonormal, (((0,), (0,)), ((), ())), precision...  38.5 us
    reduce_scatter x1, waiting for transfers between devices, shards(): lax.psum_scatter(lax.dot_general(columns, orthonormal, (((0,), (0,)), (()...  36.2 us
    all_gather x1, waiting for transfers between devices, shards(): lax.all_gather(right_factor, 'fsdp', axis=0, tiled=True)  35.9 us
  transfers between devices with their start and end apart: 12, of which 12 were waited for; matrix products, arithmetic and copies ran while one was open for 0% of the time, Pallas kernels for 0%

profile of v1, /device:TPU:0, one launch (start us, length us, event | category | flops | bytes accessed | tf_op | source)
XLA Modules:
  0.0 540.6 jit_solution(3499361927108548478)
XLA Ops:
  7.9 35.9 %all-gather.2.cloned.1.call-done = f32[2304,256]{1,0:T(8,128)} async-done(((f32[288,256]{1,0:T(8,128)}), f32[2304,256]{1,0:T(8,128)}) %all-gather.2.cloned.1.call-update) | async-done | bytes 2359312 | tf_op jit(solution)/shard_map/all_gather | solution.py:31
  43.8 22.8 %fusion.3 = f32[2304,256]{1,0:T(8,128)} fusion(f32[2304,256]{1,0:T(8,128)} %all-gather.2.cloned.1.call-done, f32[1,2304,2304]{2,1,0:T(8,128)} %param.3, bf16[1,2304,2304]{2,1,0:T(8,128)(2,1)} %param.4), kind=kOutput, calls=%fused_computation.7 | convolution fusion | flops 16318070784 | bytes 36569088 | tf_op jit(solution)/shard_map/dot_general | solution.py:29
  66.7 73.2 %all-reduce.5.cloned.1.call-done = f32[2304,256]{1,0:T(8,128)} async-done(((f32[2304,256]{1,0:T(8,128)}), f32[2304,256]{1,0:T(8,128)}) %all-reduce.5.cloned.1.call-update) | async-done | bytes 2359312 | tf_op jit(solution)/shard_map/psum | solution.py:35
  139.9 7.1 %fusion.25 = f32[256,256]{0,1:T(8,128)} fusion(f32[2304,256]{1,0:T(8,128)} %all-reduce.5.cloned.1.call-done), kind=kOutput, calls=%fused_computation.68 | convolution fusion | flops 1811939328 | bytes 2621440 | tf_op jit(solution)/shard_map/dot_general | solution.py:36
  147.3 55.3 %all-reduce.7.cloned.1.call-done = f32[256,256]{0,1:T(8,128)} async-done(((f32[256,256]{0,1:T(8,128)}), f32[256,256]{0,1:T(8,128)}) %all-reduce.7.cloned.1.call-update) | async-done | bytes 262160 | tf_op jit(solution)/shard_map/psum | solution.py:39
  204.7 11.7 %cholesky.50 = f32[128,128]{1,0:T(8,128)S(1)} custom-call(f32[128,128]{1,0:T(8,128)S(1)} %cholesky.118), custom_call_target="Cholesky" | custom-call | tf_op jit(solution)/shard_map/jit(cholesky)/cholesky | solution.py:40
  216.4 9.8 %custom-call.15 = f32[1,128,128]{1,2,0:T(8,128)S(1)} custom-call(f32[1,128,128]{2,1,0:T(8,128)S(1)} %get-tuple-element.24), custom_call_target="InvertDiagBlocksLowerTriangular" | custom-call | tf_op jit(solution)/shard_map/jit(cholesky)/cholesky | solution.py:40
  226.8 11.7 %cholesky.105 = f32[128,128]{1,0:T(8,128)S(1)} custom-call(f32[128,128]{1,0:T(8,128)S(1)} %convolution_subtract_fusion.1), custom_call_target="Cholesky" | custom-call | tf_op jit(solution)/shard_map/jit(cholesky)/cholesky | solution.py:40
  240.6 4.4 while.1
  245.0 20.3 %custom-call.16 = f32[2,128,128]{1,2,0:T(8,128)} custom-call(f32[2,128,128]{2,1,0:T(8,128)S(1)} %get-tuple-element.10), custom_call_target="InvertDiagBlocksLowerTriangular" | custom-call | tf_op jit(solution)/shard_map/jit(_solve_triangular)/triangular_solve | solution.py:41
  265.3 2.1 fusion.10
  267.4 2.9 convolution_subtract_fusion
  271.4 38.5 %fusion.1 = f32[2304,256]{1,0:T(8,128)} fusion(f32[1,2304,2304]{2,1,0:T(8,128)} %param.3, bf16[1,2304,2304]{2,1,0:T(8,128)(2,1)} %param.4, f32[128,2304]{1,0:T(8,128)S(1)} %fusion.15, f32[128,2304]{1,0:T(8,128)S(1)} %fusion.10), kind=kOutput, calls=%fused_computation.5 | convolution fusion | flops 16318660608 | bytes 36569088 | tf_op jit(solution)/shard_map/dot_general | solution.py:44
  309.9 36.2 %reduce-scatter.2.cloned.1.call-done = f32[288,256]{1,0:T(8,128)} async-done(((f32[2304,256]{1,0:T(8,128)}), f32[288,256]{1,0:T(8,128)}) %reduce-scatter.2.cloned.1.call-update) | async-done | bytes 294928 | tf_op jit(solution)/shard_map/reduce_scatter | solution.py:43
  346.2 45.1 %all-reduce.9.cloned.1.call-done = f32[288,256]{1,0:T(8,128)} async-done(((f32[288,256]{1,0:T(8,128)}), f32[288,256]{1,0:T(8,128)}) %all-reduce.9.cloned.1.call-update) | async-done | bytes 294928 | tf_op jit(solution)/shard_map/psum | solution.py:55
  392.4 7.9 %collective-permute-done = f32[288,256]{1,0:T(8,128)S(1)} collective-permute-done((f32[288,256]{1,0:T(8,128)S(1)}, f32[288,256]{1,0:T(8,128)S(1)}, u32[]{:S(2)}, u32[]{:S(2)}) %collective-permute-start) | collective-permute-done | bytes 294944 | tf_op jit(solution)/shard_map/ppermute | solution.py:19
  400.3 7.9 %collective-permute-done.1 = f32[288,256]{1,0:T(8,128)S(1)} collective-permute-done((f32[288,256]{1,0:T(8,128)S(1)}, f32[288,256]{1,0:T(8,128)S(1)}, u32[]{:S(2)}, u32[]{:S(2)}) %collective-permute-start.1) | collective-permute-done | bytes 294944 | tf_op jit(solution)/shard_map/ppermute | solution.py:19
  408.3 7.9 %collective-permute-done.2 = f32[288,256]{1,0:T(8,128)S(1)} collective-permute-done((f32[288,256]{1,0:T(8,128)S(1)}, f32[288,256]{1,0:T(8,128)S(1)}, u32[]{:S(2)}, u32[]{:S(2)}) %collective-permute-start.2) | collective-permute-done | bytes 294944 | tf_op jit(solution)/shard_map/ppermute | solution.py:19
  416.2 7.9 %collective-permute-done.3 = f32[288,256]{1,0:T(8,128)S(1)} collective-permute-done((f32[288,256]{1,0:T(8,128)S(1)}, f32[288,256]{1,0:T(8,128)S(1)}, u32[]{:S(2)}, u32[]{:S(2)}) %collective-permute-start.3) | collective-permute-done | bytes 294944 | tf_op jit(solution)/shard_map/ppermute | solution.py:19
  424.9 7.9 %collective-permute-done.4 = f32[288,256]{1,0:T(8,128)S(1)} collective-permute-done((f32[288,256]{1,0:T(8,128)S(1)}, f32[288,256]{1,0:T(8,128)S(1)}, u32[]{:S(2)}, u32[]{:S(2)}) %collective-permute-start.4) | collective-permute-done | bytes 294944 | tf_op jit(solution)/shard_map/ppermute | solution.py:19
  433.5 8.0 %collective-permute-done.5 = f32[288,256]{1,0:T(8,128)} collective-permute-done((f32[288,256]{1,0:T(8,128)S(1)}, f32[288,256]{1,0:T(8,128)}, u32[]{:S(2)}, u32[]{:S(2)}) %collective-permute-start.5) | collective-permute-done | bytes 294944 | tf_op jit(solution)/shard_map/ppermute | solution.py:19
  441.6 8.3 %collective-permute-done.6 = f32[288,256]{1,0:T(8,128)} collective-permute-done((f32[288,256]{1,0:T(8,128)}, f32[288,256]{1,0:T(8,128)}, u32[]{:S(2)}, u32[]{:S(2)}) %collective-permute-start.6) | collective-permute-done | bytes 294944 | tf_op jit(solution)/shard_map/ppermute | solution.py:19
  456.5 40.8 %fusion.5 = f32[1,2304,2304]{2,1,0:T(8,128)} fusion(f32[1,2304,2304]{2,1,0:T(8,128)} %param.3, bf16[1,2304,2304]{2,1,0:T(8,128)(2,1)} %param.4, f32[4608,256]{1,0:T(8,128)S(1)} %constant_dynamic-update-slice_fusion, s32[]{:T(128)S(6)} %select_n.19, f32[128,2304]{1,0:T(8,128)S(1)} %fusion.15, f32[128,2304]{1,0:T(8,128)S(1)} %fusion.10), kind=kOutput, calls=%fused_computation.10 | convolution fusion | flops 16329277440 | bytes 57802756 | tf_op jit(solution)/shard_map/dot_general | solution.py:59
  497.3 35.6 %fusion.6 = bf16[2304,2304]{1,0:T(8,128)(2,1)} fusion(f32[4608,256]{1,0:T(8,128)S(1)} %constant_dynamic-update-slice_fusion, s32[]{:T(128)S(6)} %select_n.19, f32[128,2304]{1,0:T(8,128)S(1)} %fusion.15, f32[128,2304]{1,0:T(8,128)S(1)} %fusion.10, f32[256]{0:T(256)S(1)} %add_sqrt_fusion), kind=kOutput, calls=%fused_computation.11 | convolution fusion | flops 16319250432 | bytes 15336452 | tf_op jit(solution)/shard_map/dot_general | solution.py:67
  (73 shorter events, 19.5 us)
Async XLA Ops:
  7.2 36.6 %all-gather.2.cloned.1.call-start = ((), (), s32[]{:S(2)}) async-start(), calls=%async_computation.1 | async-start | bytes 2654208 | tf_op jit(solution)/shard_map/all_gather | solution.py:31
  7.9 132.0 %all-reduce.5.cloned.1.call-start = ((), (), s32[]{:S(2)}) async-start(), calls=%async_computation.2 | async-start | bytes 4718592 | tf_op jit(solution)/shard_map/psum | solution.py:35
  66.6 136.0 %all-reduce.7.cloned.1.call-start = ((), (), s32[]{:S(2)}) async-start(), calls=%async_computation.3 | async-start | bytes 524288 | tf_op jit(solution)/shard_map/psum | solution.py:39
  139.9 125.4 %copy-start = (f32[2304,256]{1,0:T(8,128)S(1)}, f32[2304,256]{1,0:T(8,128)}, u32[]{:S(2)}) copy-start(f32[2304,256]{1,0:T(8,128)} %all-reduce.5.cloned.1.call-done) | copy-start | bytes 7077892
  147.0 199.2 %reduce-scatter.2.cloned.1.call-start = ((), (), s32[]{:S(2)}) async-start(), calls=%async_computation.4 | async-start | bytes 2654208 | tf_op jit(solution)/shard_map/reduce_scatter | solution.py:43
  245.0 20.3 %copy-start.2 = (f32[256,256]{1,0:T(8,128)}, f32[256,256]{1,0:T(8,128)S(1)}, u32[]{:S(2)}) copy-start(f32[256,256]{1,0:T(8,128)S(1)} %get-tuple-element.85) | copy-start | bytes 786436
  265.3 5.0 copy-start.7
  309.9 81.3 %all-reduce.9.cloned.1.call-start = ((), (), s32[]{:S(2)}) async-start(), calls=%async_computation.5 | async-start | bytes 589824 | tf_op jit(solution)/shard_map/psum | solution.py:55
  391.3 62.6 %copy-start.1 = (f32[288,256]{1,0:T(8,128)S(1)}, f32[288,256]{1,0:T(8,128)}, u32[]{:S(2)}) copy-start(f32[288,256]{1,0:T(8,128)} %all-reduce.9.cloned.1.call-done) | copy-start | bytes 884740
  392.3 8.0 %collective-permute-start = (f32[288,256]{1,0:T(8,128)S(1)}, f32[288,256]{1,0:T(8,128)S(1)}, u32[]{:S(2)}, u32[]{:S(2)}) collective-permute-start(f32[288,256]{1,0:T(8,128)S(1)} %broadcast_multiply_fusion), channel_id=1, source_target_pairs={{0,1},{1,2},{2,3},{3,4},{4,5},{5,6},{6,7},{7,0},{8,9},{9,10},{10,1... | collective-permute-start | bytes 884744 | tf_op jit(solution)/shard_map/ppermute | solution.py:19
  400.3 7.9 %collective-permute-start.1 = (f32[288,256]{1,0:T(8,128)S(1)}, f32[288,256]{1,0:T(8,128)S(1)}, u32[]{:S(2)}, u32[]{:S(2)}) collective-permute-start(f32[288,256]{1,0:T(8,128)S(1)} %collective-permute-done), channel_id=1, source_target_pairs={{0,1},{1,2},{2,3},{3,4},{4,5},{5,6},{6,7},{7,0},{8,9},{9,10},{10,1... | collective-permute-start | bytes 884744 | tf_op jit(solution)/shard_map/ppermute | solution.py:19
  408.3 7.9 %collective-permute-start.2 = (f32[288,256]{1,0:T(8,128)S(1)}, f32[288,256]{1,0:T(8,128)S(1)}, u32[]{:S(2)}, u32[]{:S(2)}) collective-permute-start(f32[288,256]{1,0:T(8,128)S(1)} %collective-permute-done.1), channel_id=1, source_target_pairs={{0,1},{1,2},{2,3},{3,4},{4,5},{5,6},{6,7},{7,0},{8,9},{9,10},{10,1... | collective-permute-start | bytes 884744 | tf_op jit(solution)/shard_map/ppermute | solution.py:19
  416.2 7.9 %collective-permute-start.3 = (f32[288,256]{1,0:T(8,128)S(1)}, f32[288,256]{1,0:T(8,128)S(1)}, u32[]{:S(2)}, u32[]{:S(2)}) collective-permute-start(f32[288,256]{1,0:T(8,128)S(1)} %collective-permute-done.2), channel_id=1, source_target_pairs={{0,1},{1,2},{2,3},{3,4},{4,5},{5,6},{6,7},{7,0},{8,9},{9,10},{10,1... | collective-permute-start | bytes 884744 | tf_op jit(solution)/shard_map/ppermute | solution.py:19
  424.1 0.7 copy-start.3
  424.9 7.9 %collective-permute-start.4 = (f32[288,256]{1,0:T(8,128)S(1)}, f32[288,256]{1,0:T(8,128)S(1)}, u32[]{:S(2)}, u32[]{:S(2)}) collective-permute-start(f32[288,256]{1,0:T(8,128)S(1)} %collective-permute-done.3), channel_id=1, source_target_pairs={{0,1},{1,2},{2,3},{3,4},{4,5},{5,6},{6,7},{7,0},{8,9},{9,10},{10,1... | collective-permute-start | bytes 884744 | tf_op jit(solution)/shard_map/ppermute | solution.py:19
  432.8 0.7 copy-start.5
  433.5 8.1 %collective-permute-start.5 = (f32[288,256]{1,0:T(8,128)S(1)}, f32[288,256]{1,0:T(8,128)}, u32[]{:S(2)}, u32[]{:S(2)}) collective-permute-start(f32[288,256]{1,0:T(8,128)S(1)} %collective-permute-done.4), channel_id=1, source_target_pairs={{0,1},{1,2},{2,3},{3,4},{4,5},{5,6},{6,7},{7,0},{8,9},{9,10},{10,1... | collective-permute-start | bytes 884744 | tf_op jit(solution)/shard_map/ppermute | solution.py:19
  441.6 8.3 %collective-permute-start.6 = (f32[288,256]{1,0:T(8,128)}, f32[288,256]{1,0:T(8,128)}, u32[]{:S(2)}, u32[]{:S(2)}) collective-permute-start(f32[288,256]{1,0:T(8,128)} %collective-permute-done.5), channel_id=1, source_target_pairs={{0,1},{1,2},{2,3},{3,4},{4,5},{5,6},{6,7},{7,0},{8,9},{9,10},{10,1... | collective-permute-start | bytes 884744 | tf_op jit(solution)/shard_map/ppermute | solution.py:19
  441.6 14.3 %copy-start.6 = (f32[288,256]{1,0:T(8,128)S(1)}, f32[288,256]{1,0:T(8,128)}, u32[]{:S(2)}) copy-start(f32[288,256]{1,0:T(8,128)} %copy-done.5) | copy-start | bytes 884740
  441.6 14.3 %copy-start.4 = (f32[288,256]{1,0:T(8,128)S(1)}, f32[288,256]{1,0:T(8,128)}, u32[]{:S(2)}) copy-start(f32[288,256]{1,0:T(8,128)} %copy-done.3) | copy-start | bytes 884740
Sparse Core Ops, SparseCore 0:
  9.6 34.1 all-gather.1
  66.8 73.0 all-reduce.4
  147.1 55.4 all-reduce.6
  310.0 36.0 reduce-scatter.1
  349.0 42.2 all-reduce.8
